TPU v7x, 32 devices: a whole 2x2x4 slice. The times are simulated.
32 devices in a mesh: shadow: 16 (over z, y, core), vocab: 2 (over x).
Axes of the slice: x: 2, y: 2, z: 4, core: 2. Of those that a mesh axis runs over, the one named last changes fastest.
Arguments:
- hidden: bfloat16 [64, 128, 2048], P('shadow'), may hold values from -18 to 18
- targets: int32 [128], replicated, may hold values from 0 to 4095
- membership: int32 [64, 4], P('shadow'), may hold values from 0 to 1, as said below
- unembedding: bfloat16 [4096, 2048], P(('shadow', 'vocab')), may hold values from -1 to 1
Outputs:
- score: float32 [64, 128], P('shadow', 'vocab')
Inputs may be any that keep to these rules, and one draw needn't show every extreme that they name: `membership`: each candidate sequence is a member of exactly 32 of the shadow models.
All inputs are finite; a program needn't handle non-finite values.
Results may differ from a plain program's by a relative error of at most 0.00055.
Values may be sent and summed in bfloat16 or wider, within the bound.
A program may use at most 64 MiB of HBM per device.

v0:
```python
import functools

import jax
import jax.numpy as jnp
from jax import lax
from jax.experimental import pallas as pl
from jax.experimental.pallas import tpu as pltpu
from jax.sharding import PartitionSpec as P

SEQ = 32
NEG_FILL = -1e30
VAR_FLOOR = 0.5
MESH = pl.DeviceIdType.MESH

HEAD_CHUNKS = 4
HIDDEN_CHUNKS = 8


def kernel(
    nsh,
    nv,
    seq,
    hidden_hbm,
    targets_hbm,
    member_hbm,
    head_hbm,
    out_ref,
    targets_ref,
    member_ref,
    hid,
    heads,
    top,
    tot,
    tgt,
    acc,
    outs,
    stat_send,
    stat_recv,
    mom_send,
    mom_recv,
    load_sem,
    up_send,
    down_send,
    line_recv,
    sib_send,
    sib_recv,
    hy_send,
    hy_recv,
    hx_send,
    hx_recv,
    st_send,
    st_recv,
    mo_send,
    mo_recv,
    ou_send,
    ou_recv,
):
    nz = nsh // 4
    chunks, head_rows, slab = heads.shape[0], heads.shape[3], heads.shape[4]
    rows = hid.shape[1]
    tokens = targets_ref.shape[1]
    group = rows // tokens
    piece = rows // nv
    hparts = hy_send.shape[0]
    part = piece // hparts

    me = lax.axis_index("shadow")
    v = lax.axis_index("vocab")
    z, y, c = me // 4, (me // 2) % 2, me % 2
    sibling = me + 1 - 2 * c
    across = me + 2 - 4 * y
    has_up, has_down = z + 1 < nz, z >= 1
    one, zero = jnp.int32(1), jnp.int32(0)

    load_head = [
        pltpu.make_async_copy(
            head_hbm.at[:, pl.ds(j * slab, slab)], heads.at[j, z, c], load_sem.at[j]
        )
        for j in range(chunks)
    ]
    load_hidden = pltpu.make_async_copy(hidden_hbm, hid.at[0], load_sem.at[chunks])
    load_small = [
        pltpu.make_async_copy(targets_hbm, targets_ref, load_sem.at[chunks + 1]),
        pltpu.make_async_copy(member_hbm, member_ref, load_sem.at[chunks + 2]),
    ]
    for copy in load_head + [load_hidden] + load_small:
        copy.start()

    barrier = pltpu.get_barrier_semaphore()

    def greet(s, w):
        pl.semaphore_signal(barrier, inc=1, device_id=(s, w), device_id_type=MESH)

    greet(sibling, v)
    greet(across, v)
    for d in range(1, nv):
        greet(me, (v + d) % nv)

    @pl.when(has_up)
    def _():
        greet(me + 4, v)

    @pl.when(has_down)
    def _():
        greet(me - 4, v)

    top[...] = jnp.full_like(top, NEG_FILL)
    tot[...] = jnp.zeros_like(tot)
    tgt[...] = jnp.zeros_like(tgt)
    pl.semaphore_wait(
        barrier, nv + 1 + jnp.where(has_up, one, zero) + jnp.where(has_down, one, zero)
    )

    def line(block, j, send, target):
        return pltpu.make_async_remote_copy(
            src_ref=heads.at[j, block, c],
            dst_ref=heads.at[j, block, c],
            send_sem=send.at[block, j],
            recv_sem=line_recv.at[block, j],
            device_id=(target, v),
            device_id_type=MESH,
        )

    def side(block, j, core):
        return pltpu.make_async_remote_copy(
            src_ref=heads.at[j, block, core],
            dst_ref=heads.at[j, block, core],
            send_sem=sib_send.at[block, j],
            recv_sem=sib_recv.at[block, j],
            device_id=(sibling, v),
            device_id_type=MESH,
        )

    def over_y(i):
        where = pl.ds(pl.multiple_of(v * piece + i * part, part), part)
        return pltpu.make_async_remote_copy(
            src_ref=hid.at[0, where],
            dst_ref=hid.at[1, where],
            send_sem=hy_send.at[i],
            recv_sem=hy_recv.at[i],
            device_id=(across, v),
            device_id_type=MESH,
        )

    def over_x(d, i, owner):
        where = pl.ds(pl.multiple_of(owner * piece + i * part, part), part)
        return pltpu.make_async_remote_copy(
            src_ref=hid.at[1, where],
            dst_ref=hid.at[1, where],
            send_sem=hx_send.at[d - 1, i],
            recv_sem=hx_recv.at[d - 1, i],
            device_id=(me, (v + d) % nv),
            device_id_type=MESH,
        )

    for j in range(chunks):
        load_head[j].wait()

        @pl.when(has_up)
        def _():
            line(z, j, up_send, me + 4).start()

        @pl.when(has_down)
        def _():
            line(z, j, down_send, me - 4).start()

        side(z, j, c).start()
    load_hidden.wait()
    for i in range(hparts):
        over_y(i).start()

    for copy in load_small:
        copy.wait()
    wanted = targets_ref[...]
    lane = lax.broadcasted_iota(jnp.int32, (group, tokens), 1)
    members = member_ref[...].astype(jnp.float32)
    spread = jnp.zeros((group, tokens), jnp.float32)
    for e in range(members.shape[1]):
        spread = jnp.where(lane // seq == e, 1.0 - members[:, e : e + 1], spread)
    outs[0] = spread
    share_outs = pltpu.make_async_remote_copy(
        src_ref=outs.at[0],
        dst_ref=outs.at[1],
        send_sem=ou_send.at[0],
        recv_sem=ou_recv.at[0],
        device_id=(across, v),
        device_id_type=MESH,
    )
    share_outs.start()

    def product(which, block, j):
        words = heads[j, block].reshape(2 * head_rows, slab)
        where = pl.ds(pl.multiple_of(j * slab, slab), slab)
        return lax.dot_general(
            words,
            hid[which, :, where],
            (((1,), (1,)), ((), ())),
            preferred_element_type=jnp.float32,
        )

    def absorb(row0, logits, block):
        count = logits.shape[0]
        i = lax.broadcasted_iota(jnp.int32, (count, tokens), 0)
        first = (block + i // (2 * head_rows)) * 4 + y * 2 + i // head_rows % 2
        ids = (first * nv + v) * head_rows + i % head_rows
        hit = ids == wanted
        for s in range(logits.shape[1] // tokens):
            row = pl.ds(row0 + s, 1)
            mine = logits[:, s * tokens : (s + 1) * tokens]
            tgt[row] += jnp.sum(jnp.where(hit, mine, 0.0), axis=0, keepdims=True)
            others = jnp.where(hit, NEG_FILL, mine)
            before = top[row]
            raised = jnp.maximum(before, jnp.max(others, axis=0, keepdims=True))
            terms = jnp.sum(jnp.exp(others - raised), axis=0, keepdims=True)
            tot[row] = tot[row] * jnp.exp(before - raised) + terms
            top[row] = raised

    def fold_blocks(block, count, which, start, size):
        words = jnp.concatenate(
            [
                heads[j, pl.ds(block, count)].reshape(count * 2 * head_rows, slab)
                for j in range(chunks)
            ],
            axis=1,
        )
        logits = lax.dot_general(
            words,
            hid[which, pl.ds(start, size)],
            (((1,), (1,)), ((), ())),
            preferred_element_type=jnp.float32,
        )
        absorb(which * group + start // tokens, logits, block)

    def whole_block(which, block):
        fold_blocks(block, 1, which, 0, rows)

    def from_sibling(block):
        def one_wait(j, _):
            side(block, j, 1 - c).wait_recv()
            return 0

        lax.fori_loop(0, chunks, one_wait, 0)

    def fold_step(k):
        @pl.when(z - k >= 0)
        def _():
            from_sibling(z - k)
            whole_block(0, z - k)

        @pl.when((k > 0) & (z + k < nz))
        def _():
            from_sibling(z + k)
            whole_block(0, z + k)

    def arrive(k, j):
        low, high = z - k, z + k

        @pl.when(low >= 0)
        def _():
            line(low, j, up_send, me).wait_recv()

            @pl.when(has_up)
            def _():
                line(low, j, up_send, me + 4).start()

            side(low, j, c).start()

        @pl.when(high < nz)
        def _():
            line(high, j, down_send, me).wait_recv()

            @pl.when(has_down)
            def _():
                line(high, j, down_send, me - 4).start()

            side(high, j, c).start()

    last = nz - 1
    early = (last - 1) * chunks
    pace = max(1, min(2, early // hparts))

    def turn(r, _):
        arrive(1 + r // chunks, r % chunks)

        @pl.when((r % pace == pace - 1) & (r // pace < hparts))
        def _():
            i = r // pace
            over_y(i).wait_recv()
            for d in range(1, nv):
                over_x(d, i, v).start()

        @pl.when(r % chunks == 0)
        def _():
            fold_step(r // chunks)

        return 0

    lax.fori_loop(0, early, turn, 0)

    at_end = (z == 0) | (z == last)
    final = jnp.where(z == 0, jnp.int32(last), zero)
    middle = chunks // 2
    by_piece = piece % tokens == 0
    unit = piece if by_piece else rows
    base = jnp.where(z == last, one, zero)
    acc[...] = jnp.zeros_like(acc)

    def closing(j, _):
        arrive(last, j)

        @pl.when(j == 0)
        def _():
            fold_step(last - 1)

        def catch_up(owner):
            start = pl.multiple_of(owner * unit, unit)
            fold_blocks(base, last, 1, start, unit)

            @pl.when(jnp.logical_not(at_end))
            def _():
                fold_blocks(last, 1, 1, start, unit)

        if by_piece:

            @pl.when(j == 0)
            def _():
                catch_up(v)

        @pl.when(j == middle)
        def _():
            for d in range(1, nv):
                for i in range(hparts):
                    over_x(d, i, (v + nv - d) % nv).wait_recv()
                if by_piece:
                    catch_up((v + nv - d) % nv)
            if not by_piece:
                catch_up(zero)

            @pl.when(at_end)
            def _():
                def missed(i, _):
                    acc[1] += product(1, final, i)
                    return 0

                lax.fori_loop(0, middle - 1, missed, 0)

        @pl.when(at_end & (j >= 1))
        def _():
            side(final, j - 1, 1 - c).wait_recv()
            acc[0] += product(0, final, j - 1)

            @pl.when(j >= middle)
            def _():
                acc[1] += product(1, final, j - 1)

        return 0

    lax.fori_loop(0, chunks, closing, 0)

    @pl.when(at_end)
    def _():
        side(final, chunks - 1, 1 - c).wait_recv()
        for which in range(2):
            absorb(which * group, acc[which] + product(which, final, chunks - 1), final)

    stat_send[0] = top[...]
    stat_send[1] = tot[...]
    stat_send[2] = tgt[...]

    offsets = [(dy, d) for dy in range(2) for d in range(nv) if dy or d]

    def stats(dy, d):
        return pltpu.make_async_remote_copy(
            src_ref=stat_send,
            dst_ref=stat_recv.at[dy * nv + d],
            send_sem=st_send.at[dy * nv + d],
            recv_sem=st_recv.at[dy * nv + d],
            device_id=(across if dy else me, (v + d) % nv),
            device_id_type=MESH,
        )

    for dy, d in offsets:
        stats(dy, d).start()

    share_outs.wait_recv()
    outside = jnp.concatenate([outs[0], outs[1]], axis=0)

    def seen(slot, which):
        value = stat_recv[slot, which]
        return pltpu.roll(value, group, 0) if slot >= nv else value

    highest, summed, target_logit = top[...], tot[...], tgt[...]
    for dy, d in offsets:
        stats(dy, d).wait_recv()
        slot = dy * nv + d
        theirs = seen(slot, 0)
        raised = jnp.maximum(highest, theirs)
        summed = summed * jnp.exp(highest - raised) + seen(slot, 1) * jnp.exp(theirs - raised)
        highest = raised
        target_logit = target_logit + seen(slot, 2)
    confidence = target_logit - (highest + jnp.log(summed))
    weighted = outside * confidence
    squared = weighted * confidence

    mom_send[0:1] = jnp.sum(weighted, axis=0, keepdims=True)
    mom_send[1:2] = jnp.sum(squared, axis=0, keepdims=True)

    around = [(dz, dc) for dz in range(nz) for dc in range(2) if dz or dc]

    def moments(dz, dc):
        column = (z + dz) % nz * 4 + y * 2 + (c + dc) % 2
        return pltpu.make_async_remote_copy(
            src_ref=mom_send,
            dst_ref=mom_recv.at[2 * dz + dc],
            send_sem=mo_send.at[2 * dz + dc],
            recv_sem=mo_recv.at[2 * dz + dc],
            device_id=(column, v),
            device_id_type=MESH,
        )

    for dz, dc in around:
        moments(dz, dc).start()
    total = mom_send[0:2]
    for dz, dc in around:
        moments(dz, dc).wait_recv()
        total = total + mom_recv[2 * dz + dc, 0:2]
    first_moment, second_moment = total[0:1], total[1:2]
    out_count = (group * nsh) // 2 - outside
    out_mean = (first_moment - weighted) / out_count
    out_variance = (second_moment - squared) / out_count - out_mean * out_mean
    score = (confidence - out_mean) * lax.rsqrt(jnp.maximum(out_variance, 0.0) + VAR_FLOOR)
    keep = tokens // nv
    shifted = pltpu.roll(score, (nv - v) % nv * keep, 1)
    out_ref[...] = shifted[0:group, 0:keep]

    def drain(block, _):
        for j in range(chunks):
            side(block, j, c).wait_send()

            @pl.when((block <= z) & has_up)
            def _():
                line(block, j, up_send, me).wait_send()

            @pl.when((block >= z) & has_down)
            def _():
                line(block, j, down_send, me).wait_send()

        return 0

    lax.fori_loop(0, nz, drain, 0)
    for i in range(hparts):
        over_y(i).wait_send()
        for d in range(1, nv):
            over_x(d, i, v).wait_send()
    for dy, d in offsets:
        stats(dy, d).wait_send()
    for dz, dc in around:
        moments(dz, dc).wait_send()
    share_outs.wait_send()


def per_device(nsh, nv, hidden, targets, membership, unembedding):
    group, tokens, width = hidden.shape
    head_rows = unembedding.shape[0]
    rows = group * tokens
    nz = nsh // 4
    chunks = HEAD_CHUNKS
    hparts = max(1, min(HIDDEN_CHUNKS, rows // nv // 16))
    dma = pltpu.SemaphoreType.DMA
    hbm, vmem = pl.BlockSpec(memory_space=pltpu.HBM), pl.BlockSpec(memory_space=pltpu.VMEM)
    return pl.pallas_call(
        functools.partial(kernel, nsh, nv, SEQ),
        out_shape=jax.ShapeDtypeStruct((group, tokens // nv), jnp.float32),
        in_specs=[hbm] * 4,
        out_specs=vmem,
        scratch_shapes=[
            pltpu.VMEM((1, tokens), jnp.int32),
            pltpu.VMEM(membership.shape, jnp.int32),
            pltpu.VMEM((2, rows, width), jnp.bfloat16),
            pltpu.VMEM((chunks, nz, 2, head_rows, width // chunks), jnp.bfloat16),
            pltpu.VMEM((2 * group, tokens), jnp.float32),
            pltpu.VMEM((2 * group, tokens), jnp.float32),
            pltpu.VMEM((2 * group, tokens), jnp.float32),
            pltpu.VMEM((2, 2 * head_rows, rows), jnp.float32),
            pltpu.VMEM((2, group, tokens), jnp.float32),
            pltpu.VMEM((3, 2 * group, tokens), jnp.float32),
            pltpu.VMEM((2 * nv, 3, 2 * group, tokens), jnp.float32),
            pltpu.VMEM((8, tokens), jnp.float32),
            pltpu.VMEM((2 * nz, 8, tokens), jnp.float32),
            dma((chunks + 3,)),
            dma((nz, chunks)),
            dma((nz, chunks)),
            dma((nz, chunks)),
            dma((nz, chunks)),
            dma((nz, chunks)),
            dma((hparts,)),
            dma((hparts,)),
            dma((max(1, nv - 1), hparts)),
            dma((max(1, nv - 1), hparts)),
            dma((2 * nv,)),
            dma((2 * nv,)),
            dma((2 * nz,)),
            dma((2 * nz,)),
            dma((1,)),
            dma((1,)),
        ],
        compiler_params=pltpu.CompilerParams(
            collective_id=0, has_side_effects=True, vmem_limit_bytes=67043328
        ),
    )(hidden.reshape(rows, width), targets.reshape(1, tokens), membership, unembedding)


def solution(mesh):
    nsh, nv = mesh.shape["shadow"], mesh.shape["vocab"]
    return jax.shard_map(
        functools.partial(per_device, nsh, nv),
        mesh=mesh,
        in_specs=(P("shadow", None, None), P(), P("shadow", None), P(("shadow", "vocab"), None)),
        out_specs=P("shadow", "vocab"),
        check_vma=False,
    )
```

profile of v0, /device:TPU:0, one launch (start us, length us, event | category | flops | bytes accessed | tf_op | source)
XLA Modules:
  0.0 52.6 jit_solution(14569866340084020582)
XLA Ops:
  0.0 51.4 %shard_map.46 = f32[4,64]{1,0:T(4,128)} custom-call(bf16[512,2048]{1,0:T(8,128)(2,1)} %bitcast.2, s32[1,128]{1,0:T(1,128)} %bitcast.3, s32[4,4]{1,0:T(4,128)} %member_hbm.1, bf16[128,2048]{1,0:T(8,128)(2,1)} %head_hbm.1), custom_call_target="tpu_custom_call" | custom-call | tf_op jit(solution)/shard_map/pallas_call | solution.py:471
  51.4 1.3 %copy.6 = f32[4,64]{1,0:T(4,128)} copy(f32[4,64]{1,0:T(4,128)} %shard_map.46) | data formatting | bytes 2048
where the time goes:
time: 52.8 us; the launch traced here: 52.6 us
  Pallas kernels  51.4 us (97%)
  local copies, waits for them, and re-layouts  1.26 us (2%)
    pallas_call x1, Pallas kernels, per_device(): pl.pallas_call(functools.partial(kernel, nsh, nv, SEQ), out_shape=jax.Sha...  51.4 us
    unnamed x1, local copies, waits for them, and re-layouts  1.26 us

commit v1 on v0

--- a/solution.py
+++ b/solution.py
@@ -39,8 +39,7 @@
     mom_send,
     mom_recv,
     load_sem,
-    up_send,
-    down_send,
+    line_send,
     line_recv,
     sib_send,
     sib_recv,
@@ -56,12 +55,12 @@
     ou_recv,
 ):
     nz = nsh // 4
-    chunks, head_rows, slab = heads.shape[0], heads.shape[3], heads.shape[4]
+    chunks, head_rows, slab = heads.shape[1], heads.shape[2], heads.shape[3]
     rows = hid.shape[1]
     tokens = targets_ref.shape[1]
     group = rows // tokens
     piece = rows // nv
-    hparts = hy_send.shape[0]
+    hparts = hy_recv.shape[0]
     part = piece // hparts
 
     me = lax.axis_index("shadow")
@@ -71,10 +70,13 @@
     across = me + 2 - 4 * y
     has_up, has_down = z + 1 < nz, z >= 1
     one, zero = jnp.int32(1), jnp.int32(0)
+    last = nz - 1
+    at_end = (z == 0) | (z == last)
+    final = jnp.where(z == 0, jnp.int32(last), zero)
 
     load_head = [
         pltpu.make_async_copy(
-            head_hbm.at[:, pl.ds(j * slab, slab)], heads.at[j, z, c], load_sem.at[j]
+            head_hbm.at[:, pl.ds(j * slab, slab)], heads.at[2 * z + c, j], load_sem.at[j]
         )
         for j in range(chunks)
     ]
@@ -111,11 +113,11 @@
         barrier, nv + 1 + jnp.where(has_up, one, zero) + jnp.where(has_down, one, zero)
     )
 
-    def line(block, j, send, target):
+    def line(block, j, target):
         return pltpu.make_async_remote_copy(
-            src_ref=heads.at[j, block, c],
-            dst_ref=heads.at[j, block, c],
-            send_sem=send.at[block, j],
+            src_ref=heads.at[2 * block + c, j],
+            dst_ref=heads.at[2 * block + c, j],
+            send_sem=line_send.at[0],
             recv_sem=line_recv.at[block, j],
             device_id=(target, v),
             device_id_type=MESH,
@@ -123,10 +125,10 @@
 
     def side(block, j, core):
         return pltpu.make_async_remote_copy(
-            src_ref=heads.at[j, block, core],
-            dst_ref=heads.at[j, block, core],
-            send_sem=sib_send.at[block, j],
-            recv_sem=sib_recv.at[block, j],
+            src_ref=heads.at[2 * block + core, j],
+            dst_ref=heads.at[2 * block + core, j],
+            send_sem=sib_send.at[0],
+            recv_sem=sib_recv.at[jnp.where(at_end & (block == final), nz + j, block)],
             device_id=(sibling, v),
             device_id_type=MESH,
         )
@@ -136,7 +138,7 @@
         return pltpu.make_async_remote_copy(
             src_ref=hid.at[0, where],
             dst_ref=hid.at[1, where],
-            send_sem=hy_send.at[i],
+            send_sem=hy_send.at[0],
             recv_sem=hy_recv.at[i],
             device_id=(across, v),
             device_id_type=MESH,
@@ -147,8 +149,8 @@
         return pltpu.make_async_remote_copy(
             src_ref=hid.at[1, where],
             dst_ref=hid.at[1, where],
-            send_sem=hx_send.at[d - 1, i],
-            recv_sem=hx_recv.at[d - 1, i],
+            send_sem=hx_send.at[0],
+            recv_sem=hx_recv.at[d - 1],
             device_id=(me, (v + d) % nv),
             device_id_type=MESH,
         )
@@ -158,11 +160,11 @@
 
         @pl.when(has_up)
         def _():
-            line(z, j, up_send, me + 4).start()
+            line(z, j, me + 4).start()
 
         @pl.when(has_down)
         def _():
-            line(z, j, down_send, me - 4).start()
+            line(z, j, me - 4).start()
 
         side(z, j, c).start()
     load_hidden.wait()
@@ -189,7 +191,7 @@
     share_outs.start()
 
     def product(which, block, j):
-        words = heads[j, block].reshape(2 * head_rows, slab)
+        words = heads[pl.ds(2 * block, 2), j].reshape(2 * head_rows, slab)
         where = pl.ds(pl.multiple_of(j * slab, slab), slab)
         return lax.dot_general(
             words,
@@ -218,7 +220,7 @@
     def fold_blocks(block, count, which, start, size):
         words = jnp.concatenate(
             [
-                heads[j, pl.ds(block, count)].reshape(count * 2 * head_rows, slab)
+                heads[pl.ds(2 * block, 2 * count), j].reshape(count * 2 * head_rows, slab)
                 for j in range(chunks)
             ],
             axis=1,
@@ -235,11 +237,8 @@
         fold_blocks(block, 1, which, 0, rows)
 
     def from_sibling(block):
-        def one_wait(j, _):
-            side(block, j, 1 - c).wait_recv()
-            return 0
-
-        lax.fori_loop(0, chunks, one_wait, 0)
+        whole = heads.at[2 * block + 1 - c]
+        pltpu.make_async_copy(whole, whole, sib_recv.at[block]).wait()
 
     def fold_step(k):
         @pl.when(z - k >= 0)
@@ -257,25 +256,24 @@
 
         @pl.when(low >= 0)
         def _():
-            line(low, j, up_send, me).wait_recv()
+            line(low, j, me).wait_recv()
 
             @pl.when(has_up)
             def _():
-                line(low, j, up_send, me + 4).start()
+                line(low, j, me + 4).start()
 
             side(low, j, c).start()
 
         @pl.when(high < nz)
         def _():
-            line(high, j, down_send, me).wait_recv()
+            line(high, j, me).wait_recv()
 
             @pl.when(has_down)
             def _():
-                line(high, j, down_send, me - 4).start()
+                line(high, j, me - 4).start()
 
             side(high, j, c).start()
 
-    last = nz - 1
     early = (last - 1) * chunks
     pace = max(1, min(2, early // hparts))
 
@@ -297,8 +295,6 @@
 
     lax.fori_loop(0, early, turn, 0)
 
-    at_end = (z == 0) | (z == last)
-    final = jnp.where(z == 0, jnp.int32(last), zero)
     middle = chunks // 2
     by_piece = piece % tokens == 0
     unit = piece if by_piece else rows
@@ -329,8 +325,9 @@
         @pl.when(j == middle)
         def _():
             for d in range(1, nv):
-                for i in range(hparts):
-                    over_x(d, i, (v + nv - d) % nv).wait_recv()
+                theirs = pl.ds(pl.multiple_of((v + nv - d) % nv * piece, piece), piece)
+                came = hid.at[1, theirs]
+                pltpu.make_async_copy(came, came, hx_recv.at[d - 1]).wait()
                 if by_piece:
                     catch_up((v + nv - d) % nv)
             if not by_piece:
@@ -373,8 +370,8 @@
         return pltpu.make_async_remote_copy(
             src_ref=stat_send,
             dst_ref=stat_recv.at[dy * nv + d],
-            send_sem=st_send.at[dy * nv + d],
-            recv_sem=st_recv.at[dy * nv + d],
+            send_sem=st_send.at[0],
+            recv_sem=st_recv.at[0],
             device_id=(across if dy else me, (v + d) % nv),
             device_id_type=MESH,
         )
@@ -390,8 +387,9 @@
         return pltpu.roll(value, group, 0) if slot >= nv else value
 
     highest, summed, target_logit = top[...], tot[...], tgt[...]
+    stat_all = stat_recv.at[pl.ds(1, 2 * nv - 1)]
+    pltpu.make_async_copy(stat_all, stat_all, st_recv.at[0]).wait()
     for dy, d in offsets:
-        stats(dy, d).wait_recv()
         slot = dy * nv + d
         theirs = seen(slot, 0)
         raised = jnp.maximum(highest, theirs)
@@ -412,8 +410,8 @@
         return pltpu.make_async_remote_copy(
             src_ref=mom_send,
             dst_ref=mom_recv.at[2 * dz + dc],
-            send_sem=mo_send.at[2 * dz + dc],
-            recv_sem=mo_recv.at[2 * dz + dc],
+            send_sem=mo_send.at[0],
+            recv_sem=mo_recv.at[0],
             device_id=(column, v),
             device_id_type=MESH,
         )
@@ -421,8 +419,9 @@
     for dz, dc in around:
         moments(dz, dc).start()
     total = mom_send[0:2]
+    mom_all = mom_recv.at[pl.ds(1, 2 * nz - 1)]
+    pltpu.make_async_copy(mom_all, mom_all, mo_recv.at[0]).wait()
     for dz, dc in around:
-        moments(dz, dc).wait_recv()
         total = total + mom_recv[2 * dz + dc, 0:2]
     first_moment, second_moment = total[0:1], total[1:2]
     out_count = (group * nsh) // 2 - outside
@@ -433,29 +432,22 @@
     shifted = pltpu.roll(score, (nv - v) % nv * keep, 1)
     out_ref[...] = shifted[0:group, 0:keep]
 
-    def drain(block, _):
-        for j in range(chunks):
-            side(block, j, c).wait_send()
-
-            @pl.when((block <= z) & has_up)
-            def _():
-                line(block, j, up_send, me).wait_send()
-
-            @pl.when((block >= z) & has_down)
-            def _():
-                line(block, j, down_send, me).wait_send()
-
-        return 0
-
-    lax.fori_loop(0, nz, drain, 0)
-    for i in range(hparts):
-        over_y(i).wait_send()
-        for d in range(1, nv):
-            over_x(d, i, v).wait_send()
-    for dy, d in offsets:
-        stats(dy, d).wait_send()
-    for dz, dc in around:
-        moments(dz, dc).wait_send()
+    def drained(ref, sem):
+        pltpu.make_async_copy(ref, ref, sem.at[0]).wait()
+
+    @pl.when(at_end)
+    def _():
+        drained(heads.at[pl.ds(0, 1)], line_send)
+
+    @pl.when(jnp.logical_not(at_end))
+    def _():
+        drained(heads.at[pl.ds(0, nz + 1)], line_send)
+
+    drained(heads.at[pl.ds(0, nz)], sib_send)
+    drained(hid.at[0, pl.ds(0, piece)], hy_send)
+    drained(hid.at[0, pl.ds(0, (nv - 1) * piece)], hx_send)
+    drained(stat_all, st_send)
+    drained(mom_all, mo_send)
     share_outs.wait_send()
 
 
@@ -470,14 +462,14 @@
     hbm, vmem = pl.BlockSpec(memory_space=pltpu.HBM), pl.BlockSpec(memory_space=pltpu.VMEM)
     return pl.pallas_call(
         functools.partial(kernel, nsh, nv, SEQ),
-        out_shape=jax.ShapeDtypeStruct((group, tokens // nv), jnp.float32),
+        out_shape=pltpu.VMEM((group, tokens // nv), jnp.float32),
         in_specs=[hbm] * 4,
         out_specs=vmem,
         scratch_shapes=[
             pltpu.VMEM((1, tokens), jnp.int32),
             pltpu.VMEM(membership.shape, jnp.int32),
             pltpu.VMEM((2, rows, width), jnp.bfloat16),
-            pltpu.VMEM((chunks, nz, 2, head_rows, width // chunks), jnp.bfloat16),
+            pltpu.VMEM((2 * nz, chunks, head_rows, width // chunks), jnp.bfloat16),
             pltpu.VMEM((2 * group, tokens), jnp.float32),
             pltpu.VMEM((2 * group, tokens), jnp.float32),
             pltpu.VMEM((2 * group, tokens), jnp.float32),
@@ -488,24 +480,23 @@
             pltpu.VMEM((8, tokens), jnp.float32),
             pltpu.VMEM((2 * nz, 8, tokens), jnp.float32),
             dma((chunks + 3,)),
+            dma((1,)),
             dma((nz, chunks)),
-            dma((nz, chunks)),
-            dma((nz, chunks)),
-            dma((nz, chunks)),
-            dma((nz, chunks)),
+            dma((1,)),
+            dma((nz + chunks,)),
+            dma((1,)),
             dma((hparts,)),
-            dma((hparts,)),
-            dma((max(1, nv - 1), hparts)),
-            dma((max(1, nv - 1), hparts)),
-            dma((2 * nv,)),
-            dma((2 * nv,)),
-            dma((2 * nz,)),
-            dma((2 * nz,)),
+            dma((1,)),
+            dma((max(1, nv - 1),)),
+            dma((1,)),
+            dma((1,)),
+            dma((1,)),
+            dma((1,)),
             dma((1,)),
             dma((1,)),
         ],
         compiler_params=pltpu.CompilerParams(
-            collective_id=0, has_side_effects=True, vmem_limit_bytes=67043328
+            collective_id=0, has_side_effects=True, vmem_limit_bytes=67035136
         ),
     )(hidden.reshape(rows, width), targets.reshape(1, tokens), membership, unembedding)
 

time: 52.8 us -> 50.5 us (0.956)
  Pallas kernels: 51.4 us -> 49.8 us
  local copies, waits for them, and re-layouts: 1.26 us -> 0.58 us
    pallas_call x1, Pallas kernels: 51.4 us -> 49.8 us  [per_device(): pl.pallas_call(functools.partial(kernel, nsh, nv, SEQ), out_shape=pltpu.V...]
    unnamed x1, local copies, waits for them, and re-layouts: 1.26 us -> 0.58 us
where the time goes in v1:
time: 50.5 us; the launch traced here: 50.4 us
  Pallas kernels  49.8 us (99%)
  local copies, waits for them, and re-layouts  0.58 us (1%)
    pallas_call x1, Pallas kernels, per_device(): pl.pallas_call(functools.partial(kernel, nsh, nv, SEQ), out_shape=pltpu.V...  49.8 us

profile of v1, /device:TPU:0, one launch (start us, length us, event | category | flops | bytes accessed | tf_op | source)
XLA Modules:
  0.0 50.4 jit_solution(11353516574357888300)
XLA Ops:
  0.0 49.8 %shard_map.46 = f32[4,64]{1,0:T(4,128)S(1)} custom-call(bf16[512,2048]{1,0:T(8,128)(2,1)} %bitcast.2, s32[1,128]{1,0:T(1,128)} %bitcast.3, s32[4,4]{1,0:T(4,128)} %member_hbm.1, bf16[128,2048]{1,0:T(8,128)(2,1)} %head_hbm.1), custom_call_target="tpu_custom_call" | custom-call | tf_op jit(solution)/shard_map/pallas_call | solution.py:463
  49.8 0.6 %copy.6 = f32[4,64]{1,0:T(4,128)} copy(f32[4,64]{1,0:T(4,128)S(1)} %shard_map.46) | data formatting | bytes 2048

commit v2 on v1

v2 whole, which is shorter than its diff:
```python
import functools

import jax
import jax.numpy as jnp
from jax import lax
from jax.experimental import pallas as pl
from jax.experimental.pallas import tpu as pltpu
from jax.sharding import PartitionSpec as P

SEQ = 32
LANES = 128
NEG_FILL = -1e30
VAR_FLOOR = 0.5
MESH = pl.DeviceIdType.MESH

SLABS = 8
PIECES = ((0, 3), (3, 6), (6, 7), (7, 8))
HIDDEN_PARTS = 8


def kernel(
    nsh,
    nv,
    splits,
    seq,
    hidden_hbm,
    targets_hbm,
    member_hbm,
    head_hbm,
    out_ref,
    targets_ref,
    member_ref,
    want,
    hid,
    heads,
    top,
    tot,
    tgt,
    acc,
    outs,
    stat_send,
    stat_recv,
    mom_send,
    mom_recv,
    load_sem,
    line_send,
    line_recv,
    sib_send,
    sib_recv,
    hy_send,
    hy_recv,
    hx_send,
    hx_recv,
    hs_send,
    hs_recv,
    st_send,
    st_recv,
    mo_send,
    mo_recv,
    ou_send,
    ou_recv,
):
    nz = nsh // 4
    last = nz - 1
    slabs, head_rows, slab = heads.shape[1], heads.shape[2], heads.shape[3]
    rows = hid.shape[1]
    tokens = targets_ref.shape[1]
    group = rows // tokens
    piece = rows // nv
    hparts = hy_recv.shape[0]
    part = piece // hparts
    pieces = len(PIECES)
    sub = tokens // splits
    per_row = LANES // sub
    depth = group * sub // LANES
    strips = rows // LANES

    me = lax.axis_index("shadow")
    v = lax.axis_index("vocab")
    z, y, c = me // 4, (me // 2) % 2, me % 2
    far = 1 - y
    sibling = me + 1 - 2 * c
    across = me + 2 - 4 * y
    has_up, has_down = z + 1 < nz, z >= 1
    one, zero = jnp.int32(1), jnp.int32(0)
    at_end = (z == 0) | (z == last)
    final = jnp.where(z == 0, jnp.int32(last), zero)
    my_split = v if splits > 1 else zero

    load_head = [
        pltpu.make_async_copy(
            head_hbm.at[:, pl.ds(s * slab, slab)], heads.at[2 * z + c, s], load_sem.at[j]
        )
        for j, (a, b) in enumerate(PIECES)
        for s in range(a, b)
    ]
    load_hidden = [
        pltpu.make_async_copy(
            hidden_hbm.at[pl.ds(s * tokens + h * sub, sub)],
            hid.at[y, pl.ds((h * group + s) * sub, sub)],
            load_sem.at[pieces],
        )
        for h in range(splits)
        for s in range(group)
    ]
    load_small = [
        pltpu.make_async_copy(targets_hbm, targets_ref, load_sem.at[pieces + 1]),
        pltpu.make_async_copy(member_hbm, member_ref, load_sem.at[pieces + 2]),
    ]
    for copy in load_head + load_hidden + load_small:
        copy.start()

    barrier = pltpu.get_barrier_semaphore()

    def greet(s, w):
        pl.semaphore_signal(barrier, inc=1, device_id=(s, w), device_id_type=MESH)

    greet(sibling, v)
    greet(across, v)
    for d in range(1, nv):
        greet(me, (v + d) % nv)

    @pl.when(has_up)
    def _():
        greet(me + 4, v)

    @pl.when(has_down)
    def _():
        greet(me - 4, v)

    top[...] = jnp.full_like(top, NEG_FILL)
    tot[...] = jnp.zeros_like(tot)
    tgt[...] = jnp.zeros_like(tgt)
    pl.semaphore_wait(
        barrier, nv + 1 + jnp.where(has_up, one, zero) + jnp.where(has_down, one, zero)
    )

    def landed(ref, sem):
        pltpu.make_async_copy(ref, ref, sem).wait()

    def line(block, j, target):
        a, b = PIECES[j]
        where = heads.at[2 * block + c, pl.ds(a, b - a)]
        return pltpu.make_async_remote_copy(
            src_ref=where,
            dst_ref=where,
            send_sem=line_send.at[0],
            recv_sem=line_recv.at[block, j],
            device_id=(target, v),
            device_id_type=MESH,
        )

    def side(block, j):
        a, b = PIECES[j]
        where = heads.at[2 * block + c, pl.ds(a, b - a)]
        return pltpu.make_async_remote_copy(
            src_ref=where,
            dst_ref=where,
            send_sem=sib_send.at[0],
            recv_sem=sib_recv.at[block],
            device_id=(sibling, v),
            device_id_type=MESH,
        )

    def over_y(slot, i):
        where = pl.ds(pl.multiple_of(v * piece + i * part, part), part)
        return pltpu.make_async_remote_copy(
            src_ref=hid.at[slot, where],
            dst_ref=hid.at[slot, where],
            send_sem=hy_send.at[0],
            recv_sem=hy_recv.at[i],
            device_id=(across, v),
            device_id_type=MESH,
        )

    def over_x(d, i):
        where = pl.ds(pl.multiple_of(v * piece + i * part, part), part)
        return pltpu.make_async_remote_copy(
            src_ref=hid.at[far, where],
            dst_ref=hid.at[far, where],
            send_sem=hx_send.at[0],
            recv_sem=hx_recv.at[d - 1],
            device_id=(me, (v + d) % nv),
            device_id_type=MESH,
        )

    def to_sibling(slot, where, index):
        return pltpu.make_async_remote_copy(
            src_ref=hid.at[slot, where],
            dst_ref=hid.at[2 + slot, where],
            send_sem=hs_send.at[0],
            recv_sem=hs_recv.at[index],
            device_id=(sibling, v),
            device_id_type=MESH,
        )

    for j, (a, b) in enumerate(PIECES):
        landed(heads.at[2 * z + c, pl.ds(a, b - a)], load_sem.at[j])

        @pl.when(has_up)
        def _():
            line(z, j, me + 4).start()

        @pl.when(has_down)
        def _():
            line(z, j, me - 4).start()

        side(z, j).start()
    landed(hid.at[y], load_sem.at[pieces])
    for i in range(hparts):
        over_y(y, i).start()

    everything = pl.ds(0, rows)

    @pl.when(at_end)
    def _():
        to_sibling(y, everything, 0).start()

    for copy in load_small:
        copy.wait()
    lane = lax.broadcasted_iota(jnp.int32, (1, LANES), 1)
    ids_wanted = targets_ref[...]
    for q in range(strips):
        h = q // depth
        row = ids_wanted
        for k in range(per_row):
            moved = pltpu.roll(ids_wanted, (k - h) * sub % LANES, 1)
            row = jnp.where(lane // sub == k, moved, row)
        want[q : q + 1] = row
    members = member_ref[...].astype(jnp.float32)
    strip = lax.broadcasted_iota(jnp.int32, (depth, LANES), 0)
    place = lax.broadcasted_iota(jnp.int32, (depth, LANES), 1)
    shadow = strip * per_row + place // sub
    example = (my_split * sub + place % sub) // seq
    spread = jnp.zeros((depth, LANES), jnp.float32)
    for s in range(group):
        for e in range(members.shape[1]):
            spread = jnp.where(
                (shadow == s) & (example == e), 1.0 - members[s : s + 1, e : e + 1], spread
            )
    outs[y] = spread
    share_outs = pltpu.make_async_remote_copy(
        src_ref=outs.at[y],
        dst_ref=outs.at[y],
        send_sem=ou_send.at[0],
        recv_sem=ou_recv.at[0],
        device_id=(across, v),
        device_id_type=MESH,
    )
    share_outs.start()

    def absorb(row0, logits, ids):
        for s in range(logits.shape[1] // LANES):
            row = pl.ds(row0 + s, 1)
            hit = ids == want[pl.ds((row0 + s) % strips, 1)]
            mine = logits[:, s * LANES : (s + 1) * LANES]
            tgt[row] += jnp.sum(jnp.where(hit, mine, 0.0), axis=0, keepdims=True)
            others = jnp.where(hit, NEG_FILL, mine)
            before = top[row]
            raised = jnp.maximum(before, jnp.max(others, axis=0, keepdims=True))
            terms = jnp.sum(jnp.exp(others - raised), axis=0, keepdims=True)
            tot[row] = tot[row] * jnp.exp(before - raised) + terms
            top[row] = raised

    def columns(which, slot, where, a, b):
        return lax.dot_general(
            jnp.concatenate([which(s) for s in range(a, b)], axis=1),
            hid[slot, where, a * slab : b * slab],
            (((1,), (1,)), ((), ())),
            preferred_element_type=jnp.float32,
        )

    def fold_blocks(block, count, slot, start, size):
        height = count * 2 * head_rows

        def words(s):
            return heads[pl.ds(2 * block, 2 * count), s].reshape(height, slab)

        logits = columns(words, slot, pl.ds(start, size), 0, slabs)
        i = lax.broadcasted_iota(jnp.int32, (height, LANES), 0)
        first = (block + i // (2 * head_rows)) * 4 + y * 2 + i // head_rows % 2
        ids = (first * nv + v) * head_rows + i % head_rows
        absorb(slot * strips + start // LANES, logits, ids)

    def fold_own(block):
        landed(heads.at[2 * block + 1 - c], sib_recv.at[block])
        fold_blocks(block, 1, y, 0, rows)

    def fold_step(k):
        @pl.when(z - k >= 0)
        def _():
            fold_own(z - k)

        @pl.when((k > 0) & (z + k < nz))
        def _():
            fold_own(z + k)

    def arrive(k, j):
        low, high = z - k, z + k

        @pl.when(low >= 0)
        def _():
            line(low, j, me).wait_recv()

            @pl.when(has_up)
            def _():
                line(low, j, me + 4).start()

            side(low, j).start()

        @pl.when(high < nz)
        def _():
            line(high, j, me).wait_recv()

            @pl.when(has_down)
            def _():
                line(high, j, me - 4).start()

            side(high, j).start()

    early = (last - 1) * pieces
    pace = max(1, min(2, early // hparts))

    def turn(k, _):
        for j in range(pieces):
            r = (k - 1) * pieces + j
            arrive(k, j)

            @pl.when((r % pace == pace - 1) & (r // pace < hparts))
            def _():
                i = r // pace
                over_y(far, i).wait_recv()
                for d in range(1, nv):
                    over_x(d, i).start()

            if j == 0:
                fold_step(k - 1)
        return 0

    lax.fori_loop(1, last, turn, 0)

    by_piece = piece % LANES == 0
    unit = piece if by_piece else rows

    def other_piece(d):
        return pl.ds(pl.multiple_of((v + nv - d) % nv * piece, piece), piece)

    def from_x():
        for d in range(1, nv):
            landed(hid.at[far, other_piece(d)], hx_recv.at[d - 1])

    def catch_up(block, count, owner):
        start = pl.multiple_of(owner * unit, unit)
        fold_blocks(block, count, far, start, unit)

    def catch_rest(block, count):
        if by_piece:
            for d in range(1, nv):
                catch_up(block, count, (v + nv - d) % nv)
        else:
            catch_up(block, count, zero)

    @pl.when(jnp.logical_not(at_end))
    def _():
        fold_step(last - 1)
        if by_piece:
            catch_up(zero, nz, v)
        from_x()
        catch_rest(zero, nz)

    @pl.when(at_end)
    def _():
        base = jnp.where(z == last, one, zero)
        mine = pl.ds(pl.multiple_of(v * piece, piece), piece)
        to_sibling(far, mine, 1).start()
        fold_step(last - 1)
        if by_piece:
            catch_up(base, last, v)

        def words(s):
            return heads[2 * final + c, s]

        def came(j):
            line(final, j, me).wait_recv()

        def product(j, slot):
            return columns(words, slot, everything, *PIECES[j])

        came(0)
        landed(hid.at[2 + y], hs_recv.at[0])
        for slot in (y, 2 + y):
            acc[slot] = product(0, slot)
        from_x()
        for d in range(1, nv):
            to_sibling(far, other_piece(d), 1).start()
        catch_rest(base, last)
        landed(hid.at[2 + far], hs_recv.at[1])
        for slot in (far, 2 + far):
            acc[slot] = product(0, slot)
        for j in range(1, pieces - 1):
            came(j)
            for slot in range(4):
                acc[slot] += product(j, slot)
        came(pieces - 1)
        i = lax.broadcasted_iota(jnp.int32, (head_rows, LANES), 0)
        ids = ((final * 4 + y * 2 + c) * nv + v) * head_rows + i
        for slot in range(4):
            absorb(slot * strips, acc[slot] + product(pieces - 1, slot), ids)

    summed = tot[...]
    partial = jnp.where(summed > 0.0, top[...] + jnp.log(summed), NEG_FILL)
    for h in range(splits):
        for g in range(2):
            for w in range(2):
                a = (2 * g + w) * strips + h * depth
                stat_send[h, g, w * depth : (w + 1) * depth] = partial[a : a + depth]
                stat_send[h, g, (2 + w) * depth : (3 + w) * depth] = tgt[a : a + depth]

    mates = [
        (dc, dy, d) for dc in range(2) for dy in range(2) for d in range(nv) if dc or dy or d
    ]

    def stats(dc, dy, d):
        column = z * 4 + (y + dy) % 2 * 2 + (c + dc) % 2
        beside = (v + d) % nv
        return pltpu.make_async_remote_copy(
            src_ref=stat_send.at[beside if splits > 1 else 0, dc],
            dst_ref=stat_recv.at[(dc * 2 + dy) * nv + d],
            send_sem=st_send.at[0],
            recv_sem=st_recv.at[0],
            device_id=(column, beside),
            device_id_type=MESH,
        )

    for mate in mates:
        stats(*mate).start()

    share_outs.wait_recv()
    outside = jnp.concatenate([outs[0], outs[1]], axis=0)
    own = stat_send[my_split, 0]
    stat_all = stat_recv.at[pl.ds(1, 4 * nv - 1)]
    landed(stat_all, st_recv.at[0])
    parts = [own] + [stat_recv[(dc * 2 + dy) * nv + d] for dc, dy, d in mates]
    highest = functools.reduce(jnp.maximum, [p[0 : 2 * depth] for p in parts])
    summed = sum(jnp.exp(p[0 : 2 * depth] - highest) for p in parts)
    target_logit = sum(p[2 * depth : 4 * depth] for p in parts)
    confidence = target_logit - (highest + jnp.log(summed))
    weighted = outside * confidence
    squared = weighted * confidence

    mom_send[0:1] = jnp.sum(weighted, axis=0, keepdims=True)
    mom_send[1:2] = jnp.sum(squared, axis=0, keepdims=True)

    around = [(dz, dc) for dz in range(nz) for dc in range(2) if dz or dc]

    def moments(dz, dc):
        column = (z + dz) % nz * 4 + y * 2 + (c + dc) % 2
        return pltpu.make_async_remote_copy(
            src_ref=mom_send,
            dst_ref=mom_recv.at[2 * dz + dc],
            send_sem=mo_send.at[0],
            recv_sem=mo_recv.at[0],
            device_id=(column, v),
            device_id_type=MESH,
        )

    for dz, dc in around:
        moments(dz, dc).start()
    total = mom_send[0:2]
    mom_all = mom_recv.at[pl.ds(1, 2 * nz - 1)]
    landed(mom_all, mo_recv.at[0])
    for dz, dc in around:
        total = total + mom_recv[2 * dz + dc, 0:2]
    total = sum(pltpu.roll(total, k * sub, 1) if k else total for k in range(per_row))
    first_moment, second_moment = total[0:1], total[1:2]
    out_count = (group * nsh) // 2 - outside
    out_mean = (first_moment - weighted) / out_count
    out_variance = (second_moment - squared) / out_count - out_mean * out_mean
    score = (confidence - out_mean) * lax.rsqrt(jnp.maximum(out_variance, 0.0) + VAR_FLOOR)
    score = jnp.where(y == 0, score[0:depth], score[depth : 2 * depth])
    keep = tokens // nv
    if splits > 1:
        for s in range(group):
            p, a = s // per_row, s % per_row * sub
            out_ref[s : s + 1] = score[p : p + 1, a : a + sub]
    else:
        shifted = pltpu.roll(score, (nv - v) % nv * keep, 1)
        out_ref[...] = shifted[0:group, 0:keep]

    @pl.when(at_end)
    def _():
        landed(heads.at[pl.ds(0, 1)], line_send.at[0])
        landed(heads.at[pl.ds(0, nz - 1)], sib_send.at[0])
        landed(hid.at[pl.ds(0, 2)], hs_send.at[0])

    @pl.when(jnp.logical_not(at_end))
    def _():
        landed(heads.at[pl.ds(0, nz + 1)], line_send.at[0])
        landed(heads.at[pl.ds(0, nz)], sib_send.at[0])

    landed(hid.at[0, pl.ds(0, piece)], hy_send.at[0])
    landed(hid.at[0, pl.ds(0, (nv - 1) * piece)], hx_send.at[0])
    landed(stat_all, st_send.at[0])
    landed(mom_all, mo_send.at[0])
    share_outs.wait_send()


def per_device(nsh, nv, hidden, targets, membership, unembedding):
    group, tokens, width = hidden.shape
    head_rows = unembedding.shape[0]
    rows = group * tokens
    nz = nsh // 4
    pieces = len(PIECES)
    splits = nv if rows // nv % (2 * LANES) == 0 else 1
    depth = rows // splits // LANES
    hparts = max(1, min(HIDDEN_PARTS, rows // nv // 16, (nz - 2) * pieces))
    dma = pltpu.SemaphoreType.DMA
    hbm, vmem = pl.BlockSpec(memory_space=pltpu.HBM), pl.BlockSpec(memory_space=pltpu.VMEM)
    strips = 4 * rows // LANES
    return pl.pallas_call(
        functools.partial(kernel, nsh, nv, splits, SEQ),
        out_shape=pltpu.VMEM((group, tokens // nv), jnp.float32),
        in_specs=[hbm] * 4,
        out_specs=vmem,
        scratch_shapes=[
            pltpu.VMEM((1, tokens), jnp.int32),
            pltpu.VMEM(membership.shape, jnp.int32),
            pltpu.VMEM((rows // LANES, LANES), jnp.int32),
            pltpu.VMEM((4, rows, width), jnp.bfloat16),
            pltpu.VMEM((2 * nz, SLABS, head_rows, width // SLABS), jnp.bfloat16),
            pltpu.VMEM((strips, LANES), jnp.float32),
            pltpu.VMEM((strips, LANES), jnp.float32),
            pltpu.VMEM((strips, LANES), jnp.float32),
            pltpu.VMEM((4, head_rows, rows), jnp.float32),
            pltpu.VMEM((2, depth, LANES), jnp.float32),
            pltpu.VMEM((splits, 2, 4 * depth, LANES), jnp.float32),
            pltpu.VMEM((4 * nv, 4 * depth, LANES), jnp.float32),
            pltpu.VMEM((8, LANES), jnp.float32),
            pltpu.VMEM((2 * nz, 8, LANES), jnp.float32),
            dma((pieces + 3,)),
            dma((1,)),
            dma((nz, pieces)),
            dma((1,)),
            dma((nz,)),
            dma((1,)),
            dma((hparts,)),
            dma((1,)),
            dma((max(1, nv - 1),)),
            dma((1,)),
            dma((2,)),
            dma((1,)),
            dma((1,)),
            dma((1,)),
            dma((1,)),
            dma((1,)),
            dma((1,)),
        ],
        compiler_params=pltpu.CompilerParams(
            collective_id=0, has_side_effects=True, vmem_limit_bytes=67035136
        ),
    )(hidden.reshape(rows, width), targets.reshape(1, tokens), membership, unembedding)


def solution(mesh):
    nsh, nv = mesh.shape["shadow"], mesh.shape["vocab"]
    return jax.shard_map(
        functools.partial(per_device, nsh, nv),
        mesh=mesh,
        in_specs=(P("shadow", None, None), P(), P("shadow", None), P(("shadow", "vocab"), None)),
        out_specs=P("shadow", "vocab"),
        check_vma=False,
    )
```

time: 50.5 us -> 49 us (0.970)
  Pallas kernels: 49.8 us -> 48.3 us
    pallas_call x1, Pallas kernels: 49.8 us -> 48.3 us  [per_device(): pl.pallas_call(functools.partial(kernel, nsh, nv, splits, SEQ), out_shape...]
where the time goes in v2:
time: 49 us; the launch traced here: 48.9 us
  Pallas kernels  48.3 us (99%)
  local copies, waits for them, and re-layouts  0.58 us (1%)
    pallas_call x1, Pallas kernels, per_device(): pl.pallas_call(functools.partial(kernel, nsh, nv, splits, SEQ), out_shape...  48.3 us

profile of v2, /device:TPU:0, one launch (start us, length us, event | category | flops | bytes accessed | tf_op | source)
XLA Modules:
  0.0 48.9 jit_solution(13820190191392333114)
XLA Ops:
  0.0 48.3 %shard_map.46 = f32[4,64]{1,0:T(4,128)S(1)} custom-call(bf16[512,2048]{1,0:T(8,128)(2,1)} %bitcast.2, s32[1,128]{1,0:T(1,128)} %bitcast.3, s32[4,4]{1,0:T(4,128)} %member_hbm.1, bf16[128,2048]{1,0:T(8,128)(2,1)} %head_hbm.1), custom_call_target="tpu_custom_call" | custom-call | tf_op jit(solution)/shard_map/pallas_call | solution.py:520
  48.3 0.6 %copy.6 = f32[4,64]{1,0:T(4,128)} copy(f32[4,64]{1,0:T(4,128)S(1)} %shard_map.46) | data formatting | bytes 2048
